TPU v7x, 32 devices: a whole 2x2x4 slice. The times are simulated.
32 devices in a mesh: vox: 8 (over y, x, core), sen: 4 (over z).
Axes of the slice: x: 2, y: 2, z: 4, core: 2. Of those that a mesh axis runs over, the one named last changes fastest.
Arguments:
- image: float32 [8, 2, 512], P('vox'), may hold values from -6 to 6
- weights: bfloat16 [8, 4, 5, 1024, 1024], P('vox', 'sen'), may hold values from -0.0625 to 0.0625
- block_ids: int32 [8, 4, 5], P('vox', 'sen'), may hold values from 0 to 15
- offsets: int32 [8, 4, 5], P('vox', 'sen'), may hold values from 0 to 1984
- counts: int32 [8, 4], P('vox', 'sen'), may hold values from 1 to 5, as said below
- measured: bfloat16 [4, 256, 2048], P('sen', 'vox'), may hold values from -6 to 6
Outputs:
- image_next: float32 [8, 2, 512], P('vox')
- residual: float32 [4, 256, 2048], P('sen', 'vox')
Inputs may be any that keep to these rules, and one draw needn't show every extreme that they name: `counts`: some slab and group has all 5 slots live in every draw.
All inputs are finite; a program needn't handle non-finite values.
Results may differ from a plain program's by a relative error of at most 0.0025.
Values may be sent and summed in bfloat16 or wider, within the bound.
A program may use at most 64 MiB of HBM per device.

v0:
```python
import functools

import jax
import jax.numpy as jnp
from jax import lax
from jax.experimental import pallas as pl
from jax.experimental.pallas import tpu as pltpu
from jax.sharding import PartitionSpec as P

SB = 16
WIN = 64
LANES = 128

STEP_SIZE = 0.25
TV_WEIGHT = 0.3
TV_EPS = 0.01
C1 = 8.0 / 12.0
C2 = 1.0 / 12.0
MESH = pl.DeviceIdType.MESH


def lane_iota(shape):
    return lax.broadcasted_iota(jnp.int32, shape, len(shape) - 1)


def ahead(value, shift):
    length = value.shape[-1]
    return pltpu.roll(value, (-shift) % length, value.ndim - 1)


def stencil(value):
    return C2 * ahead(value, -2) - C1 * ahead(value, -1) + C1 * ahead(value, 1) - C2 * ahead(value, 2)


def stencil_edges(value):
    length = value.shape[-1]
    at = lane_iota(value.shape)
    total = jnp.where(at >= 2, C2 * ahead(value, -2), 0.0)
    total = total - jnp.where(at >= 1, C1 * ahead(value, -1), 0.0)
    total = total + jnp.where(at < length - 1, C1 * ahead(value, 1), 0.0)
    return total - jnp.where(at < length - 2, C2 * ahead(value, 2), 0.0)


def block_mask(width):
    row = lax.broadcasted_iota(jnp.int32, (SB, width), 0)
    return lane_iota((SB, width)) // WIN == row


def gather_kernel(
    n, slots, chunks, image_in, weights, ids_in, offs_in, counts,
    pieces_all, meta_all, halo, wbuf,
    image, ids, offs, mine, meta,
    wsem, load_sem, local_sem, small_send, small_recv, halo_send, halo_recv,
    piece_send, piece_recv,
):
    me = lax.axis_index("vox")
    voxels = weights.shape[3]
    depth = voxels // chunks
    groups = mine.shape[0]

    arguments = []
    pairs = ((ids_in, ids), (offs_in, offs), (image_in, image))
    for i, (src, dst) in enumerate(pairs):
        load = pltpu.make_async_copy(src, dst, load_sem.at[i])
        load.start()
        arguments.append(load)
    loads = []
    for k in range(slots):
        for q in range(chunks):
            part = pl.ds(q * depth, depth)
            load = pltpu.make_async_copy(weights.at[0, 0, k, part], wbuf.at[k, part], wsem.at[k, q])
            load.start()
            loads.append(load)

    barrier = pltpu.get_barrier_semaphore()
    for step in range(1, n):
        pl.semaphore_signal(barrier, inc=1, device_id={"vox": (me + step) % n}, device_id_type=MESH)
    for load in arguments:
        load.wait()
    meta[...] = jnp.where(
        lane_iota(meta.shape) == slots, jnp.full(meta.shape, counts[0, 0]), 0
    )
    meta[0:1, 0:slots] = ids[0]
    meta[1:2, 0:slots] = offs[0]
    low = image[0].astype(jnp.bfloat16)
    flat = jnp.concatenate([low[r : r + 1] for r in range(low.shape[0])], axis=1)
    flat = jnp.broadcast_to(flat, (SB, voxels))
    mask = block_mask(SB * WIN)
    alive = jnp.full((SB, LANES), counts[0, 0])
    left = lane_iota((SB, LANES)) < WIN
    pl.semaphore_wait(barrier, n - 1)

    def remote(src, dst, send, recv, target):
        return pltpu.make_async_remote_copy(
            src_ref=src, dst_ref=dst, send_sem=send, recv_sem=recv,
            device_id={"vox": target}, device_id_type=MESH,
        )

    small, sends = [], []
    for step in range(1, n):
        copy = remote(meta, meta_all.at[me], small_send.at[step], small_recv.at[step], (me + step) % n)
        copy.start()
        small.append(copy)
    own_meta = pltpu.make_async_copy(meta, meta_all.at[me], local_sem.at[0])
    own_meta.start()
    for side, target in ((0, (me + 1) % n), (1, (me + n - 1) % n)):
        copy = remote(image.at[0], halo.at[side], halo_send.at[side], halo_recv.at[side], target)
        copy.start()
        sends.append(copy)

    locals_ = [own_meta]
    packed = None
    for k in range(slots):
        total = jnp.zeros((SB, SB * WIN), jnp.float32)
        for q in range(chunks):
            loads[k * chunks + q].wait()
            total = total + jnp.dot(
                flat[:, q * depth : (q + 1) * depth],
                wbuf[k, q * depth : (q + 1) * depth],
                preferred_element_type=jnp.float32,
            )
        total = jnp.where(mask, total, 0.0)
        tile = total[:, 0:LANES]
        for g in range(1, SB * WIN // LANES):
            tile = tile + total[:, g * LANES : (g + 1) * LANES]
        tile = tile + pltpu.roll(tile, WIN, 1)
        tile = jnp.where(alive > k, tile, 0.0)
        packed = jnp.where(left, tile, 0.0) if k % 2 == 0 else jnp.where(left, packed, tile)
        if k % 2 == 1 or k == slots - 1:
            g = k // 2
            mine[g] = packed
            for step in range(1, n):
                copy = remote(
                    mine.at[g], pieces_all.at[me, g], piece_send.at[g, step], piece_recv.at[g, step],
                    (me + step) % n,
                )
                copy.start()
                sends.append(copy)
            copy = pltpu.make_async_copy(mine.at[g], pieces_all.at[me, g], local_sem.at[1 + g])
            copy.start()
            locals_.append(copy)

    for copy in locals_:
        copy.wait()
    for copy in small + sends:
        copy.wait()


def place_kernel(
    n, slots, pieces_all, meta_all, measured,
    windows, residual, signals, adjoints, table, meta_sem,
):
    me = lax.axis_index("vox")
    rows, samples = measured.shape[1:]
    tables = pltpu.make_async_copy(meta_all, table, meta_sem)
    tables.start()
    signals[...] = jnp.zeros_like(signals)
    adjoints[:, pl.ds(samples, LANES)] = jnp.zeros((adjoints.shape[0], LANES), jnp.float32)
    if rows < SB:
        adjoints[...] = jnp.zeros_like(adjoints)
    tables.wait()
    at = lane_iota((SB, LANES))

    def place(j, carry):
        for k in range(slots):
            number = table[j, 0, k]
            start = table[j, 1, k]
            shift = start % LANES
            base = pl.multiple_of((start // LANES + 1) * LANES, LANES)
            sensors = pl.ds(pl.multiple_of(number * SB, SB), SB)
            packed = pieces_all[j, k // 2]
            keep = (at < WIN) if k % 2 == 0 else (at >= WIN)
            turn = shift if k % 2 == 0 else (shift + WIN) % LANES
            piece = pltpu.roll(jnp.where(keep, packed, 0.0), turn, 1)
            signals[sensors, pl.ds(base, LANES)] += jnp.where(at >= shift, piece, 0.0)
            after = pl.multiple_of(base + LANES, LANES)
            signals[sensors, pl.ds(after, LANES)] += jnp.where(at < shift, piece, 0.0)
        return carry

    lax.fori_loop(0, n, place, 0)

    for r in range(0, rows, 8):
        line = pl.multiple_of((me * rows + r) // 8 * 8, 8)
        block = stencil_edges(signals[pl.ds(line, 8), pl.ds(LANES, samples)])
        if rows % 8 == 0:
            block = block - measured[0, r : r + 8].astype(jnp.float32)
            residual[0, r : r + 8] = block
            block = -stencil_edges(block)
        else:
            which = jnp.full((rows, samples), (me * rows) % 8)
            part = block[0:rows]
            for i in range(1, 8 // rows):
                part = jnp.where(which == i * rows, block[i * rows : (i + 1) * rows], part)
            part = part - measured[0].astype(jnp.float32)
            residual[0] = part
            part = -stencil_edges(part)
            block = jnp.concatenate(
                [jnp.where(which == i * rows, part, 0.0) for i in range(8 // rows)], axis=0
            )
        spot = r if rows >= SB else pl.multiple_of((me * rows + r) % SB // 8 * 8, 8)
        adjoints[pl.ds(spot, 8), pl.ds(0, samples)] = block

    per = max(rows // SB, 1)
    home = me * rows // SB

    def cut(j, carry):
        packed = None
        for k in range(slots):
            number = table[j, 0, k]
            start = table[j, 1, k]
            near = number - home
            mine = (near >= 0) & (near < per) & (k < table[j, 0, slots])
            line = pl.ds(pl.multiple_of(jnp.clip(near, 0, per - 1) * SB, SB), SB)
            column = pl.multiple_of(start // LANES * LANES, LANES)
            shift = start % LANES
            turn = (LANES - shift + (k % 2) * WIN) % LANES
            first = pltpu.roll(adjoints[line, pl.ds(column, LANES)], turn, 1)
            second = pltpu.roll(
                adjoints[line, pl.ds(pl.multiple_of(column + LANES, LANES), LANES)], turn, 1
            )
            window = jnp.where(at - (k % 2) * WIN < LANES - shift, first, second)
            live = jnp.full(window.shape, mine.astype(jnp.int32))
            window = jnp.where(live > 0, window, 0.0)
            packed = window if k % 2 == 0 else jnp.where(at < WIN, packed, window)
            if k % 2 == 1 or k == slots - 1:
                windows[j, k // 2] = packed.astype(windows.dtype)
        return carry

    lax.fori_loop(0, n, cut, 0)


def variation(n, place, image, halo):
    def units(volume, step_z):
        shape = volume.shape
        row = lax.broadcasted_iota(jnp.int32, shape, 0)
        below = jnp.concatenate([volume[1:], volume[shape[0] - 1 :]], axis=0)
        step_y = below - volume
        step_x = jnp.where(lane_iota(shape) < shape[1] - 1, ahead(volume, 1) - volume, 0.0)
        size = jnp.sqrt(step_z * step_z + step_y * step_y + step_x * step_x + TV_EPS)
        return step_z / size, step_y / size, step_x / size, row

    volume = image[0]
    before, after = halo[0], halo[1]
    is_first = jnp.full(volume.shape, place) == 0
    is_last = jnp.full(volume.shape, place) == n - 1
    lower_z, _, _, _ = units(before, volume - before)
    unit_z, unit_y, unit_x, row = units(volume, jnp.where(is_last, 0.0, after - volume))
    tv = jnp.where(is_first, 0.0, lower_z) - unit_z
    shifted_y = jnp.concatenate([jnp.zeros_like(unit_y[0:1]), unit_y[: unit_y.shape[0] - 1]], axis=0)
    tv = tv + shifted_y - unit_y
    tv = tv + jnp.where(lane_iota(volume.shape) >= 1, ahead(unit_x, -1), 0.0) - unit_x
    return tv


def update_kernel(
    n, ns, windows, wbuf, image, halo, out, windows_all, grad, parts, send, recv, window_send, window_recv
):
    mine = lax.axis_index("sen")
    place = lax.axis_index("vox")
    barrier = pltpu.get_barrier_semaphore()
    for step in range(1, ns):
        pl.semaphore_signal(
            barrier, inc=1, device_id={"sen": (mine + step) % ns}, device_id_type=MESH
        )
    for step in range(1, n):
        pl.semaphore_signal(
            barrier, inc=1, device_id={"vox": (place + step) % n}, device_id_type=MESH
        )
    pl.semaphore_wait(barrier, ns + n - 2)
    exchanges = []
    for step in range(1, n):
        to = (place + step) % n
        copy = pltpu.make_async_remote_copy(
            src_ref=windows.at[to], dst_ref=windows_all.at[step - 1], send_sem=window_send.at[step],
            recv_sem=window_recv.at[step], device_id={"vox": to}, device_id_type=MESH,
        )
        copy.start()
        exchanges.append(copy)
    tv = variation(n, place, image, halo)
    for copy in exchanges:
        copy.wait()
    mask = block_mask(SB * WIN)
    left = lane_iota((SB, LANES)) < WIN
    part = None
    for g in range(windows.shape[1]):
        packed = windows[place, g].astype(jnp.float32)
        for step in range(1, n):
            packed = packed + windows_all[step - 1, g].astype(jnp.float32)
        turned = pltpu.roll(packed, WIN, 1)
        for k in range(2 * g, min(2 * g + 2, wbuf.shape[0])):
            window = jnp.where(left, packed, turned) if k % 2 == 0 else jnp.where(left, turned, packed)
            spread = jnp.concatenate([window] * (SB * WIN // LANES), axis=1)
            spread = jnp.where(mask, spread, 0.0).astype(jnp.bfloat16)
            term = lax.dot_general(
                spread, wbuf[k], (((1,), (1,)), ((), ())), preferred_element_type=jnp.float32
            )
            part = term if part is None else part + term
    grad[...] = jnp.sum(part, axis=0, keepdims=True)
    copies = []
    for step in range(1, ns):
        copy = pltpu.make_async_remote_copy(
            src_ref=grad, dst_ref=parts.at[mine], send_sem=send.at[step], recv_sem=recv.at[step],
            device_id={"sen": (mine + step) % ns}, device_id_type=MESH,
        )
        copy.start()
        copies.append(copy)

    for copy in copies:
        copy.wait()
    flat = None
    for index in range(ns):
        chosen = jnp.full(grad.shape, mine) == index
        term = jnp.where(chosen, grad[...], parts[index])
        flat = term if flat is None else flat + term
    volume = image[0]
    width = volume.shape[1]
    for r in range(volume.shape[0]):
        total = flat[:, r * width : (r + 1) * width]
        out[0, r : r + 1] = volume[r : r + 1] - STEP_SIZE * (total + TV_WEIGHT * tv[r : r + 1])


def on_device(image, weights, block_ids, offsets, counts, measured):
    n = lax.axis_size("vox")
    ns = lax.axis_size("sen")
    slots, voxels, cells = weights.shape[2:]
    rows, samples = measured.shape[1:]
    groups = (slots + 1) // 2
    chunks = 4
    vmem = pl.BlockSpec(memory_space=pltpu.VMEM)
    smem = pl.BlockSpec(memory_space=pltpu.SMEM)
    hbm = pl.BlockSpec(memory_space=pltpu.HBM)
    anywhere = pl.BlockSpec(memory_space=pl.ANY)
    dma = pltpu.SemaphoreType.DMA
    shape = jax.ShapeDtypeStruct

    def pin(value):
        return pltpu.with_memory_space_constraint(value, pltpu.HBM)

    pieces_all, meta_all, halo, held = pl.pallas_call(
        functools.partial(gather_kernel, n, slots, chunks),
        out_shape=(
            shape((n, groups, SB, LANES), jnp.float32),
            shape((n, 2, LANES), jnp.int32),
            shape((2,) + image.shape[1:], jnp.float32),
            shape((slots, voxels, cells), jnp.bfloat16),
        ),
        in_specs=[hbm, hbm, hbm, hbm, smem],
        out_specs=(vmem,) * 4,
        scratch_shapes=[
            pltpu.VMEM(image.shape, jnp.float32),
            pltpu.VMEM(block_ids.shape, jnp.int32),
            pltpu.VMEM(offsets.shape, jnp.int32),
            pltpu.VMEM((groups, SB, LANES), jnp.float32),
            pltpu.VMEM((2, LANES), jnp.int32),
            dma((slots, chunks)),
            dma((3,)),
            dma((1 + groups,)),
            dma((n,)),
            dma((n,)),
            dma((2,)),
            dma((2,)),
            dma((groups, n)),
            dma((groups, n)),
        ],
        compiler_params=pltpu.CompilerParams(
            collective_id=0, has_side_effects=True, vmem_limit_bytes=16 << 20
        ),
        name="gather_kernel",
    )(pin(image), pin(weights), pin(block_ids), pin(offsets), counts)

    windows, residual = pl.pallas_call(
        functools.partial(place_kernel, n, slots),
        out_shape=(
            shape((n, groups, SB, LANES), jnp.bfloat16),
            shape(measured.shape, jnp.float32),
        ),
        in_specs=[vmem, anywhere, vmem],
        out_specs=(vmem, vmem),
        scratch_shapes=[
            pltpu.VMEM((rows * n, samples + 3 * LANES), jnp.float32),
            pltpu.VMEM((max(rows, SB), samples + LANES), jnp.float32),
            pltpu.SMEM((n, 2, LANES), jnp.int32),
            dma,
        ],
        compiler_params=pltpu.CompilerParams(vmem_limit_bytes=16 << 20),
        name="place_kernel",
    )(pieces_all, meta_all, measured)

    image_next = pl.pallas_call(
        functools.partial(update_kernel, n, ns),
        out_shape=shape(image.shape, jnp.float32),
        in_specs=[vmem] * 4,
        out_specs=vmem,
        scratch_shapes=[
            pltpu.VMEM((n - 1, groups, SB, LANES), jnp.bfloat16),
            pltpu.VMEM((1, voxels), jnp.float32),
            pltpu.VMEM((ns, 1, voxels), jnp.float32),
            dma((ns,)),
            dma((ns,)),
            dma((n,)),
            dma((n,)),
        ],
        compiler_params=pltpu.CompilerParams(
            collective_id=1, has_side_effects=True, vmem_limit_bytes=16 << 20
        ),
        name="update_kernel",
    )(windows, held, image, halo)
    return (image_next, residual)


def solution(mesh):
    placed = (
        P("vox", None, None),
        P("vox", "sen", None, None, None),
        P("vox", "sen", None),
        P("vox", "sen", None),
        P("vox", "sen"),
        P("sen", "vox", None),
    )
    return jax.shard_map(
        on_device,
        mesh=mesh,
        in_specs=placed,
        out_specs=(P("vox", None, None), P("sen", "vox", None)),
        check_vma=False,
    )
```

profile of v0, /device:TPU:0, one launch (start us, length us, event | category | flops | bytes accessed | tf_op | source)
XLA Modules:
  0.0 31.7 jit_solution(1039299710951476255)
XLA Ops:
  0.6 0.0 copy-start.1
  0.6 0.0 copy-start
  1.3 12.7 %gather_kernel.1 = (f32[8,3,16,128]{3,2,1,0:T(8,128)S(1)}, s32[8,2,128]{2,1,0:T(2,128)S(1)}, f32[2,2,512]{2,1,0:T(2,128)S(1)}, bf16[5,1024,1024]{2,1,0:T(8,128)(2,1)S(1)}) custom-call(f32[1,2,512]{2,1,0:T(2,128)} %image.1, bf16[1,1,5,1024,1024]{4,3,2,1,0:T(8,128)(2,1)} %weights.1, s32[1,1,5]{2,1,0:T(1,128)} %ids_in.1, s32[1,1,5]{2,1,0:T(1,128)} %offs_in.1, ...), custom_call_target="tpu_custom_call" | custom-call | tf_op jit(solution)/shard_map/gather_kernel/pallas_call | solution.py:339
  14.0 0.0 copy-done
  14.1 4.0 %place_kernel.1 = (bf16[8,3,16,128]{3,2,1,0:T(8,128)(2,1)S(1)}, f32[1,32,2048]{2,1,0:T(8,128)}) custom-call(f32[8,3,16,128]{3,2,1,0:T(8,128)S(1)} %get-tuple-element.8.pieces_all, s32[8,2,128]{2,1,0:T(2,128)S(1)} %get-tuple-element.9.meta_all, bf16[1,32,2048]{2,1,0:T(8,128)(2,1)S(1)} %copy-done), custom_call_target="tpu_custom_call" | custom-call | tf_op jit(solution)/shard_map/place_kernel/pallas_call | solution.py:371
  18.1 0.0 copy-done.1
  18.1 13.0 %update_kernel.1 = f32[1,2,512]{2,1,0:T(2,128)S(1)} custom-call(bf16[8,3,16,128]{3,2,1,0:T(8,128)(2,1)S(1)} %get-tuple-element.10.windows, bf16[5,1024,1024]{2,1,0:T(8,128)(2,1)S(1)} %get-tuple-element.11.wbuf, f32[1,2,512]{2,1,0:T(2,128)S(1)} %copy-done.1, f32[2,2,512]{2,1,0:T(2,128)S(1)} %get-tuple-element.12.halo), custom_call_target="tpu_custom_call" | custom-call | tf_op jit(solution)/shard_map/update_kernel/pallas_call | solution.py:389
  31.1 0.6 %copy.10 = f32[1,2,512]{2,1,0:T(2,128)} copy(f32[1,2,512]{2,1,0:T(2,128)S(1)} %update_kernel.1) | data formatting | bytes 8192
Async XLA Ops:
  0.6 17.5 %copy-start.1 = (f32[1,2,512]{2,1,0:T(2,128)S(1)}, f32[1,2,512]{2,1,0:T(2,128)}, u32[]{:S(2)}) copy-start(f32[1,2,512]{2,1,0:T(2,128)} %image.1) | copy-start | bytes 12292
  0.6 13.4 %copy-start = (bf16[1,32,2048]{2,1,0:T(8,128)(2,1)S(1)}, bf16[1,32,2048]{2,1,0:T(8,128)(2,1)}, u32[]{:S(2)}) copy-start(bf16[1,32,2048]{2,1,0:T(8,128)(2,1)} %measured.1) | copy-start | bytes 393220
where the time goes:
time: 31.9 us; the launch traced here: 31.7 us
  Pallas kernels  29.8 us (93%)
  between operations  1.37 us (4%)
  local copies, waits for them, and re-layouts  0.6 us (2%)
    pallas_call x1, Pallas kernels, on_device(): pl.pallas_call(functools.partial(update_kernel, n, ns), out_shape=shape(i...  13 us
    pallas_call x1, Pallas kernels, on_device(): pl.pallas_call(functools.partial(gather_kernel, n, slots, chunks), out_sh...  12.7 us
    pallas_call x1, Pallas kernels, on_device(): pl.pallas_call(functools.partial(place_kernel, n, slots), out_shape=(shap...  4.04 us

commit v1 on v0

--- a/solution.py
+++ b/solution.py
@@ -88,27 +88,28 @@
     mask = block_mask(SB * WIN)
     alive = jnp.full((SB, LANES), counts[0, 0])
     left = lane_iota((SB, LANES)) < WIN
-    pl.semaphore_wait(barrier, n - 1)
-
     def remote(src, dst, send, recv, target):
         return pltpu.make_async_remote_copy(
             src_ref=src, dst_ref=dst, send_sem=send, recv_sem=recv,
             device_id={"vox": target}, device_id_type=MESH,
         )
 
-    small, sends = [], []
-    for step in range(1, n):
-        copy = remote(meta, meta_all.at[me], small_send.at[step], small_recv.at[step], (me + step) % n)
-        copy.start()
-        small.append(copy)
-    own_meta = pltpu.make_async_copy(meta, meta_all.at[me], local_sem.at[0])
-    own_meta.start()
-    for side, target in ((0, (me + 1) % n), (1, (me + n - 1) % n)):
-        copy = remote(image.at[0], halo.at[side], halo_send.at[side], halo_recv.at[side], target)
-        copy.start()
-        sends.append(copy)
-
-    locals_ = [own_meta]
+    small, sends, locals_ = [], [], []
+
+    def greet():
+        pl.semaphore_wait(barrier, n - 1)
+        for step in range(1, n):
+            copy = remote(meta, meta_all.at[me], small_send.at[step], small_recv.at[step], (me + step) % n)
+            copy.start()
+            small.append(copy)
+        own_meta = pltpu.make_async_copy(meta, meta_all.at[me], local_sem.at[0])
+        own_meta.start()
+        locals_.append(own_meta)
+        for side, target in ((0, (me + 1) % n), (1, (me + n - 1) % n)):
+            copy = remote(image.at[0], halo.at[side], halo_send.at[side], halo_recv.at[side], target)
+            copy.start()
+            sends.append(copy)
+
     packed = None
     for k in range(slots):
         total = jnp.zeros((SB, SB * WIN), jnp.float32)
@@ -129,6 +130,8 @@
         if k % 2 == 1 or k == slots - 1:
             g = k // 2
             mine[g] = packed
+            if g == 0:
+                greet()
             for step in range(1, n):
                 copy = remote(
                     mine.at[g], pieces_all.at[me, g], piece_send.at[g, step], piece_recv.at[g, step],
@@ -161,9 +164,13 @@
     tables.wait()
     at = lane_iota((SB, LANES))
 
+    per = max(rows // SB, 1)
+    home = me * rows // SB
+
     def place(j, carry):
         for k in range(slots):
-            number = table[j, 0, k]
+            near = table[j, 0, k] - home
+            number = jnp.where((near >= 0) & (near < per), near, per)
             start = table[j, 1, k]
             shift = start % LANES
             base = pl.multiple_of((start // LANES + 1) * LANES, LANES)
@@ -181,7 +188,8 @@
 
     for r in range(0, rows, 8):
         line = pl.multiple_of((me * rows + r) // 8 * 8, 8)
-        block = stencil_edges(signals[pl.ds(line, 8), pl.ds(LANES, samples)])
+        near = pl.multiple_of(line - home * SB, 8)
+        block = stencil_edges(signals[pl.ds(near, 8), pl.ds(LANES, samples)])
         if rows % 8 == 0:
             block = block - measured[0, r : r + 8].astype(jnp.float32)
             residual[0, r : r + 8] = block
@@ -199,9 +207,6 @@
             )
         spot = r if rows >= SB else pl.multiple_of((me * rows + r) % SB // 8 * 8, 8)
         adjoints[pl.ds(spot, 8), pl.ds(0, samples)] = block
-
-    per = max(rows // SB, 1)
-    home = me * rows // SB
 
     def cut(j, carry):
         packed = None
@@ -377,7 +382,7 @@
         in_specs=[vmem, anywhere, vmem],
         out_specs=(vmem, vmem),
         scratch_shapes=[
-            pltpu.VMEM((rows * n, samples + 3 * LANES), jnp.float32),
+            pltpu.VMEM((max(rows, SB) + SB, samples + 3 * LANES), jnp.float32),
             pltpu.VMEM((max(rows, SB), samples + LANES), jnp.float32),
             pltpu.SMEM((n, 2, LANES), jnp.int32),
             dma,

time: 31.9 us -> 31.9 us (level)
  no operation moved by 1% of the time
where the time goes in v1:
time: 31.9 us; the launch traced here: 31.7 us
  Pallas kernels  29.8 us (93%)
  between operations  1.37 us (4%)
  local copies, waits for them, and re-layouts  0.6 us (2%)
    pallas_call x1, Pallas kernels, on_device(): pl.pallas_call(functools.partial(update_kernel, n, ns), out_shape=shape(i...  13 us
    pallas_call x1, Pallas kernels, on_device(): pl.pallas_call(functools.partial(gather_kernel, n, slots, chunks), out_sh...  12.7 us
    pallas_call x1, Pallas kernels, on_device(): pl.pallas_call(functools.partial(place_kernel, n, slots), out_shape=(shap...  4.05 us

profile of v1, /device:TPU:0, one launch (start us, length us, event | category | flops | bytes accessed | tf_op | source)
XLA Modules:
  0.0 31.7 jit_solution(7276539593407774224)
XLA Ops:
  0.6 0.0 copy-start.1
  0.6 0.0 copy-start
  1.3 12.7 %gather_kernel.1 = (f32[8,3,16,128]{3,2,1,0:T(8,128)S(1)}, s32[8,2,128]{2,1,0:T(2,128)S(1)}, f32[2,2,512]{2,1,0:T(2,128)S(1)}, bf16[5,1024,1024]{2,1,0:T(8,128)(2,1)S(1)}) custom-call(f32[1,2,512]{2,1,0:T(2,128)} %image.1, bf16[1,1,5,1024,1024]{4,3,2,1,0:T(8,128)(2,1)} %weights.1, s32[1,1,5]{2,1,0:T(1,128)} %ids_in.1, s32[1,1,5]{2,1,0:T(1,128)} %offs_in.1, ...), custom_call_target="tpu_custom_call" | custom-call | tf_op jit(solution)/shard_map/gather_kernel/pallas_call | solution.py:344
  14.0 0.0 copy-done
  14.1 4.1 %place_kernel.1 = (bf16[8,3,16,128]{3,2,1,0:T(8,128)(2,1)S(1)}, f32[1,32,2048]{2,1,0:T(8,128)}) custom-call(f32[8,3,16,128]{3,2,1,0:T(8,128)S(1)} %get-tuple-element.8.pieces_all, s32[8,2,128]{2,1,0:T(2,128)S(1)} %get-tuple-element.9.meta_all, bf16[1,32,2048]{2,1,0:T(8,128)(2,1)S(1)} %copy-done), custom_call_target="tpu_custom_call" | custom-call | tf_op jit(solution)/shard_map/place_kernel/pallas_call | solution.py:376
  18.1 0.0 copy-done.1
  18.1 13.0 %update_kernel.1 = f32[1,2,512]{2,1,0:T(2,128)S(1)} custom-call(bf16[8,3,16,128]{3,2,1,0:T(8,128)(2,1)S(1)} %get-tuple-element.10.windows, bf16[5,1024,1024]{2,1,0:T(8,128)(2,1)S(1)} %get-tuple-element.11.wbuf, f32[1,2,512]{2,1,0:T(2,128)S(1)} %copy-done.1, f32[2,2,512]{2,1,0:T(2,128)S(1)} %get-tuple-element.12.halo), custom_call_target="tpu_custom_call" | custom-call | tf_op jit(solution)/shard_map/update_kernel/pallas_call | solution.py:394
  31.1 0.6 %copy.10 = f32[1,2,512]{2,1,0:T(2,128)} copy(f32[1,2,512]{2,1,0:T(2,128)S(1)} %update_kernel.1) | data formatting | bytes 8192
Async XLA Ops:
  0.6 17.5 %copy-start.1 = (f32[1,2,512]{2,1,0:T(2,128)S(1)}, f32[1,2,512]{2,1,0:T(2,128)}, u32[]{:S(2)}) copy-start(f32[1,2,512]{2,1,0:T(2,128)} %image.1) | copy-start | bytes 12292
  0.6 13.4 %copy-start = (bf16[1,32,2048]{2,1,0:T(8,128)(2,1)S(1)}, bf16[1,32,2048]{2,1,0:T(8,128)(2,1)}, u32[]{:S(2)}) copy-start(bf16[1,32,2048]{2,1,0:T(8,128)(2,1)} %measured.1) | copy-start | bytes 393220
